TPU v7x, 128 devices: a whole 4x4x4 slice. The times are simulated.
128 devices in a mesh: blk: 32 (over x, z_lo, y), table: 4 (over z_hi, core).
Axes of the slice: x: 4, y: 4, z: 4 (z_hi: 2, z_lo: 2; z = z_hi * 2 + z_lo), core: 2. Of those that a mesh axis runs over, the one named last changes fastest.
Arguments:
- queries: bfloat16 [65536, 256], P(('blk', 'table')), may hold values from -20 to 20
- items: bfloat16 [65536, 256], P(('blk', 'table')), may hold values from -4.8 to 4.8
- positives: int32 [65536], P(('blk', 'table')), may hold values from 0 to 511
- item_owner: int32 [65536, 1], P(('blk', 'table')), may hold values from 0 to 127; in each aligned block of 512 rows (0 to 511, 512 to 1023, ...) at most 12 rows name the same one
- item_row: int32 [65536], P(('blk', 'table')), may hold values from 0 to 16383
Outputs:
- query_grad: bfloat16 [65536, 256], P(('blk', 'table'))
- item_grad: bfloat16 [65536, 256], P(('blk', 'table'))
- table_grad: bfloat16 [2097152, 256], P(('blk', 'table'))
Inputs may be any that keep to these rules, and one draw needn't show every extreme that they name: `item_owner`: among the rows of one device, no owner is named more than 12 times, a bound that some block reaches.
All inputs are finite; a program needn't handle non-finite values.
Results may differ from a plain program's by a relative error of at most 0.0034.
Values may be sent and summed in bfloat16 or wider, within the bound.
A program may use at most 64 MiB of HBM per device.

v0:
```python
import math

import jax
import jax.numpy as jnp
from jax import lax
from jax.sharding import PartitionSpec as P

ROWS_DEV = 16384


def passed_along(block, axis, distance):
    devices = range(lax.axis_size(axis))
    route = [((i - distance) % len(devices), i) for i in devices]
    return lax.ppermute(block, axis, route)


def from_everyone(value, axis):
    copies = jnp.broadcast_to(value, (lax.axis_size(axis), *value.shape))
    return lax.all_to_all(copies, axis, split_axis=0, concat_axis=0, tiled=True)


def in_order(blocks, dim):
    blocks = jnp.moveaxis(blocks, 0, dim)
    lengths = blocks.shape
    return blocks.reshape(*lengths[:dim], lengths[dim] * lengths[dim + 1], *lengths[dim + 2 :])


def gather_directly(value, axis, dim):
    blocks = from_everyone(value, axis)
    return in_order(blocks, dim)


def local(queries, items, positives, item_owner, item_row):
    size_rows, feature_width = queries.shape
    logit_scale = 3.0 / math.sqrt(feature_width)
    window = lax.axis_size("blk") // 2
    blk_count = lax.axis_size("blk")
    table_count = lax.axis_size("table")
    devices = blk_count * table_count
    capacity = 3 * size_rows // devices
    places = jnp.arange(size_rows, dtype=jnp.int32)
    positive_hot = (positives[:, None] == places[None, :]).astype(jnp.float32)

    def scores_of(query_block, item_block):
        return logit_scale * lax.dot_general(
            query_block, item_block, (((1,), (1,)), ((), ())), preferred_element_type=jnp.float32
        )

    own_scores = scores_of(queries, items)
    top_now = jnp.max(own_scores, axis=1)
    total_now = jnp.sum(jnp.exp(own_scores - top_now[:, None]), axis=1)
    visited = jnp.zeros((window, size_rows, feature_width), jnp.bfloat16)

    def forward(offset, loop_state):
        item_block, top_old, total_old, kept_blocks = loop_state
        item_block = passed_along(item_block, "blk", 1)
        scores = scores_of(queries, item_block)
        top_new = jnp.maximum(top_old, jnp.max(scores, axis=1))
        total_new = total_old * jnp.exp(top_old - top_new) + jnp.sum(
            jnp.exp(scores - top_new[:, None]), axis=1
        )
        kept_blocks = lax.dynamic_update_index_in_dim(kept_blocks, item_block, offset, 0)
        return (item_block, top_new, total_new, kept_blocks)

    last_block, top_now, total_now, visited = lax.fori_loop(
        1, window, forward, (items, top_now, total_now, visited)
    )
    log_total = top_now + jnp.log(total_now)

    def weights_of(scores, totals, subtract):
        return (jnp.exp(scores - totals[:, None]) - subtract).astype(jnp.bfloat16)

    own_weights = weights_of(own_scores, log_total, positive_hot)
    query_sum = jnp.dot(own_weights, items, preferred_element_type=jnp.float32)
    item_sum = lax.dot_general(
        own_weights, queries, (((0,), (0,)), ((), ())), preferred_element_type=jnp.float32
    )

    def visit_items(offset):
        return lax.dynamic_index_in_dim(visited, offset, 0, keepdims=False)

    all_totals = gather_directly(log_total, "blk", 0)
    my_index = lax.axis_index("blk")

    def backward(offset, loop_state):
        item_block, query_block, query_acc, item_acc = loop_state
        item_block = visit_items(offset)
        weights = weights_of(scores_of(queries, item_block), log_total, 0.0)
        query_acc = query_acc + jnp.dot(weights, item_block, preferred_element_type=jnp.float32)
        query_block = passed_along(query_block, "blk", -1)
        source = (my_index + offset) % blk_count
        their_totals = lax.dynamic_slice_in_dim(all_totals, source * size_rows, size_rows, 0)
        their_weights = weights_of(scores_of(query_block, items), their_totals, 0.0)
        item_acc = item_acc + lax.dot_general(
            their_weights, query_block, (((0,), (0,)), ((), ())), preferred_element_type=jnp.float32
        )
        return (item_block, query_block, query_acc, item_acc)

    final_block, final_queries, query_sum, item_sum = lax.fori_loop(
        1, window, backward, (items, queries, query_sum, item_sum)
    )
    item_grad = (logit_scale * item_sum).astype(jnp.bfloat16)
    query_grad = (logit_scale * query_sum).astype(jnp.bfloat16)
    owners = item_owner[:, 0]
    owner_hot = (owners[:, None] == jnp.arange(devices, dtype=jnp.int32)[None, :]).astype(
        jnp.float32
    )
    earlier = (places[:, None] > places[None, :]).astype(jnp.float32)
    before = jnp.dot(earlier, owner_hot, precision=lax.Precision.HIGHEST)
    ranks = jnp.sum(before * owner_hot, axis=1).astype(jnp.int32)
    slots = owners * capacity + ranks
    send_rows = (
        jnp.zeros((devices * capacity, feature_width), jnp.bfloat16).at[slots].set(item_grad)
    )
    send_ids = jnp.full((devices * capacity,), ROWS_DEV, jnp.int32).at[slots].set(item_row)
    got_rows, got_ids = (
        lax.all_to_all(send_rows, ("blk", "table"), split_axis=0, concat_axis=0, tiled=True),
        lax.all_to_all(send_ids, ("blk", "table"), split_axis=0, concat_axis=0, tiled=True),
    )
    table_grad = (
        jnp.zeros((ROWS_DEV, feature_width), jnp.float32)
        .at[got_ids]
        .add(got_rows.astype(jnp.float32), mode="drop")
        .astype(jnp.bfloat16)
    )
    return (query_grad, item_grad, table_grad)


def solution(mesh):
    in_specs = (
        P(("blk", "table"), None),
        P(("blk", "table"), None),
        P(("blk", "table")),
        P(("blk", "table"), None),
        P(("blk", "table")),
    )
    out_specs = (P(("blk", "table"), None), P(("blk", "table"), None), P(("blk", "table"), None))
    return jax.shard_map(local, mesh=mesh, in_specs=in_specs, out_specs=out_specs, check_vma=False)
```

profile of v0, /device:TPU:24, one launch (start us, length us, event | category | flops | bytes accessed | tf_op | source)
XLA Modules:
  0.0 453.1 jit_solution(5444579023257502993)
XLA Ops:
  4.7 173.1 %while.42 = (s32[]{:T(128)}, bf16[512,256]{1,0:T(8,128)(2,1)S(1)}, f32[512]{0:T(512)S(1)}, f32[512]{0:T(512)S(1)}, bf16[16,512,256]{2,1,0:T(8,128)(2,1)}, /*inde...) while((s32[]{:T(128)}, bf16[512,256]{1,0:T(8,128)(2,1)S(1)}, f32[512]{0:T(512)S(1)}, ...), condition=%wide.region_5.6_spmd, body=%wide.region_2.5_spmd.sunk | while | flops 135267328 | bytes 4745387 | solution.py:65
  6.4 6.5 %collective-permute-done = bf16[512,256]{1,0:T(8,128)(2,1)S(1)} collective-permute-done((bf16[512,256]{1,0:T(8,128)(2,1)S(1)}, bf16[512,256]{1,0:T(8,128)(2,1)S(1)}, u32[]{:S(2)}, u32[]{:S(2)}) %collective-permute-start) | collective-permute-done | bytes 262176 | tf_op jit(solution)/shard_map/while/body/eval_jaxpr/ppermute | solution.py:14
  14.2 3.7 collective-permute-start
  17.9 4.7 %collective-permute-done = bf16[512,256]{1,0:T(8,128)(2,1)S(1)} collective-permute-done((bf16[512,256]{1,0:T(8,128)(2,1)S(1)}, bf16[512,256]{1,0:T(8,128)(2,1)S(1)}, u32[]{:S(2)}, u32[]{:S(2)}) %collective-permute-start) | collective-permute-done | bytes 262176 | tf_op jit(solution)/shard_map/while/body/eval_jaxpr/ppermute | solution.py:14
  23.9 4.6 %collective-permute-start = (bf16[512,256]{1,0:T(8,128)(2,1)S(1)}, bf16[512,256]{1,0:T(8,128)(2,1)S(1)}, u32[]{:S(2)}, u32[]{:S(2)}) collective-permute-start(bf16[512,256]{1,0:T(8,128)(2,1)S(1)} %get-tuple-element.629), channel_id=1, source_target_pairs={{124,0},{0,4},{4,8},{8,12},{12,16},{16,20},{20,24},{24,28},{28,32}... | collective-permute-start | bytes 786440 | tf_op jit(solution)/shard_map/while/body/eval_jaxpr/ppermute | solution.py:14
  28.5 3.9 collective-permute-done
  33.7 4.6 %collective-permute-start = (bf16[512,256]{1,0:T(8,128)(2,1)S(1)}, bf16[512,256]{1,0:T(8,128)(2,1)S(1)}, u32[]{:S(2)}, u32[]{:S(2)}) collective-permute-start(bf16[512,256]{1,0:T(8,128)(2,1)S(1)} %get-tuple-element.629), channel_id=1, source_target_pairs={{124,0},{0,4},{4,8},{8,12},{12,16},{16,20},{20,24},{24,28},{28,32}... | collective-permute-start | bytes 786440 | tf_op jit(solution)/shard_map/while/body/eval_jaxpr/ppermute | solution.py:14
  38.3 3.9 collective-permute-done
  43.5 4.6 %collective-permute-start = (bf16[512,256]{1,0:T(8,128)(2,1)S(1)}, bf16[512,256]{1,0:T(8,128)(2,1)S(1)}, u32[]{:S(2)}, u32[]{:S(2)}) collective-permute-start(bf16[512,256]{1,0:T(8,128)(2,1)S(1)} %get-tuple-element.629), channel_id=1, source_target_pairs={{124,0},{0,4},{4,8},{8,12},{12,16},{16,20},{20,24},{24,28},{28,32}... | collective-permute-start | bytes 786440 | tf_op jit(solution)/shard_map/while/body/eval_jaxpr/ppermute | solution.py:14
  48.1 3.9 collective-permute-done
  53.3 4.6 %collective-permute-start = (bf16[512,256]{1,0:T(8,128)(2,1)S(1)}, bf16[512,256]{1,0:T(8,128)(2,1)S(1)}, u32[]{:S(2)}, u32[]{:S(2)}) collective-permute-start(bf16[512,256]{1,0:T(8,128)(2,1)S(1)} %get-tuple-element.629), channel_id=1, source_target_pairs={{124,0},{0,4},{4,8},{8,12},{12,16},{16,20},{20,24},{24,28},{28,32}... | collective-permute-start | bytes 786440 | tf_op jit(solution)/shard_map/while/body/eval_jaxpr/ppermute | solution.py:14
  57.9 4.3 collective-permute-done
  63.5 4.6 %collective-permute-start = (bf16[512,256]{1,0:T(8,128)(2,1)S(1)}, bf16[512,256]{1,0:T(8,128)(2,1)S(1)}, u32[]{:S(2)}, u32[]{:S(2)}) collective-permute-start(bf16[512,256]{1,0:T(8,128)(2,1)S(1)} %get-tuple-element.629), channel_id=1, source_target_pairs={{124,0},{0,4},{4,8},{8,12},{12,16},{16,20},{20,24},{24,28},{28,32}... | collective-permute-start | bytes 786440 | tf_op jit(solution)/shard_map/while/body/eval_jaxpr/ppermute | solution.py:14
  68.1 5.5 %collective-permute-done = bf16[512,256]{1,0:T(8,128)(2,1)S(1)} collective-permute-done((bf16[512,256]{1,0:T(8,128)(2,1)S(1)}, bf16[512,256]{1,0:T(8,128)(2,1)S(1)}, u32[]{:S(2)}, u32[]{:S(2)}) %collective-permute-start) | collective-permute-done | bytes 262176 | tf_op jit(solution)/shard_map/while/body/eval_jaxpr/ppermute | solution.py:14
  74.9 4.6 %collective-permute-start = (bf16[512,256]{1,0:T(8,128)(2,1)S(1)}, bf16[512,256]{1,0:T(8,128)(2,1)S(1)}, u32[]{:S(2)}, u32[]{:S(2)}) collective-permute-start(bf16[512,256]{1,0:T(8,128)(2,1)S(1)} %get-tuple-element.629), channel_id=1, source_target_pairs={{124,0},{0,4},{4,8},{8,12},{12,16},{16,20},{20,24},{24,28},{28,32}... | collective-permute-start | bytes 786440 | tf_op jit(solution)/shard_map/while/body/eval_jaxpr/ppermute | solution.py:14
  79.5 6.6 %collective-permute-done = bf16[512,256]{1,0:T(8,128)(2,1)S(1)} collective-permute-done((bf16[512,256]{1,0:T(8,128)(2,1)S(1)}, bf16[512,256]{1,0:T(8,128)(2,1)S(1)}, u32[]{:S(2)}, u32[]{:S(2)}) %collective-permute-start) | collective-permute-done | bytes 262176 | tf_op jit(solution)/shard_map/while/body/eval_jaxpr/ppermute | solution.py:14
  87.5 4.6 %collective-permute-start = (bf16[512,256]{1,0:T(8,128)(2,1)S(1)}, bf16[512,256]{1,0:T(8,128)(2,1)S(1)}, u32[]{:S(2)}, u32[]{:S(2)}) collective-permute-start(bf16[512,256]{1,0:T(8,128)(2,1)S(1)} %get-tuple-element.629), channel_id=1, source_target_pairs={{124,0},{0,4},{4,8},{8,12},{12,16},{16,20},{20,24},{24,28},{28,32}... | collective-permute-start | bytes 786440 | tf_op jit(solution)/shard_map/while/body/eval_jaxpr/ppermute | solution.py:14
  92.1 5.8 %collective-permute-done = bf16[512,256]{1,0:T(8,128)(2,1)S(1)} collective-permute-done((bf16[512,256]{1,0:T(8,128)(2,1)S(1)}, bf16[512,256]{1,0:T(8,128)(2,1)S(1)}, u32[]{:S(2)}, u32[]{:S(2)}) %collective-permute-start) | collective-permute-done | bytes 262176 | tf_op jit(solution)/shard_map/while/body/eval_jaxpr/ppermute | solution.py:14
  99.2 4.6 %collective-permute-start = (bf16[512,256]{1,0:T(8,128)(2,1)S(1)}, bf16[512,256]{1,0:T(8,128)(2,1)S(1)}, u32[]{:S(2)}, u32[]{:S(2)}) collective-permute-start(bf16[512,256]{1,0:T(8,128)(2,1)S(1)} %get-tuple-element.629), channel_id=1, source_target_pairs={{124,0},{0,4},{4,8},{8,12},{12,16},{16,20},{20,24},{24,28},{28,32}... | collective-permute-start | bytes 786440 | tf_op jit(solution)/shard_map/while/body/eval_jaxpr/ppermute | solution.py:14
  103.8 7.5 %collective-permute-done = bf16[512,256]{1,0:T(8,128)(2,1)S(1)} collective-permute-done((bf16[512,256]{1,0:T(8,128)(2,1)S(1)}, bf16[512,256]{1,0:T(8,128)(2,1)S(1)}, u32[]{:S(2)}, u32[]{:S(2)}) %collective-permute-start) | collective-permute-done | bytes 262176 | tf_op jit(solution)/shard_map/while/body/eval_jaxpr/ppermute | solution.py:14
  114.7 11.9 %collective-permute-done = bf16[512,256]{1,0:T(8,128)(2,1)S(1)} collective-permute-done((bf16[512,256]{1,0:T(8,128)(2,1)S(1)}, bf16[512,256]{1,0:T(8,128)(2,1)S(1)}, u32[]{:S(2)}, u32[]{:S(2)}) %collective-permute-start) | collective-permute-done | bytes 262176 | tf_op jit(solution)/shard_map/while/body/eval_jaxpr/ppermute | solution.py:14
  127.9 13.2 %collective-permute-done = bf16[512,256]{1,0:T(8,128)(2,1)S(1)} collective-permute-done((bf16[512,256]{1,0:T(8,128)(2,1)S(1)}, bf16[512,256]{1,0:T(8,128)(2,1)S(1)}, u32[]{:S(2)}, u32[]{:S(2)}) %collective-permute-start) | collective-permute-done | bytes 262176 | tf_op jit(solution)/shard_map/while/body/eval_jaxpr/ppermute | solution.py:14
  142.4 11.5 %collective-permute-done = bf16[512,256]{1,0:T(8,128)(2,1)S(1)} collective-permute-done((bf16[512,256]{1,0:T(8,128)(2,1)S(1)}, bf16[512,256]{1,0:T(8,128)(2,1)S(1)}, u32[]{:S(2)}, u32[]{:S(2)}) %collective-permute-start) | collective-permute-done | bytes 262176 | tf_op jit(solution)/shard_map/while/body/eval_jaxpr/ppermute | solution.py:14
  155.3 10.1 %collective-permute-done = bf16[512,256]{1,0:T(8,128)(2,1)S(1)} collective-permute-done((bf16[512,256]{1,0:T(8,128)(2,1)S(1)}, bf16[512,256]{1,0:T(8,128)(2,1)S(1)}, u32[]{:S(2)}, u32[]{:S(2)}) %collective-permute-start) | collective-permute-done | bytes 262176 | tf_op jit(solution)/shard_map/while/body/eval_jaxpr/ppermute | solution.py:14
  166.7 9.8 %collective-permute-done = bf16[512,256]{1,0:T(8,128)(2,1)S(1)} collective-permute-done((bf16[512,256]{1,0:T(8,128)(2,1)S(1)}, bf16[512,256]{1,0:T(8,128)(2,1)S(1)}, u32[]{:S(2)}, u32[]{:S(2)}) %collective-permute-start) | collective-permute-done | bytes 262176 | tf_op jit(solution)/shard_map/while/body/eval_jaxpr/ppermute | solution.py:14
  178.5 20.8 %all-to-all-start = ((f32[32,1,512]{2,1,0:T(1,128)}), f32[32,1,512]{2,1,0:T(1,128)S(1)}, u32[]{:S(2)}, u32[]{:S(2)}) async-start(f32[32,1,512]{2,1,0:T(1,128)} %broadcast_in_dim.43), calls=%async_computation | async-start | bytes 131072 | tf_op jit(solution)/shard_map/all_to_all | solution.py:19
  205.9 8.0 %all-to-all-start.1 = ((s32[128,12,1]{1,2,0:T(1,128)}), s32[128,12,1]{1,2,0:T(1,128)S(1)}, u32[]{:S(2)}, u32[]{:S(2)}) async-start(s32[128,12,1]{1,2,0:T(1,128)} %bitcast.6), calls=%async_computation.1 | async-start | bytes 131072 | tf_op jit(solution)/shard_map/all_to_all | solution.py:118
  213.9 164.9 %while.43 = (s32[]{:T(128)}, bf16[512,256]{1,0:T(8,128)(2,1)S(1)}, f32[512,256]{1,0:T(8,128)S(1)}, f32[512,256]{1,0:T(8,128)S(1)}, bf16[16,512,256]{2,1,0:T(8,12...) while((s32[]{:T(128)}, bf16[512,256]{1,0:T(8,128)(2,1)S(1)}, ...), condition=%wide.region_7.8_spmd, body=%wide.region_6.7_spmd.sunk | while | flops 538705920 | bytes 4990362 | solution.py:99
  216.7 8.0 %collective-permute-done.1 = bf16[512,256]{1,0:T(8,128)(2,1)S(1)} collective-permute-done((bf16[512,256]{1,0:T(8,128)(2,1)S(1)}, bf16[512,256]{1,0:T(8,128)(2,1)S(1)}, u32[]{:S(2)}, u32[]{:S(2)}) %collective-permute-start.1) | collective-permute-done | bytes 262176 | tf_op jit(solution)/shard_map/while/body/eval_jaxpr/ppermute | solution.py:14
  227.5 7.8 %collective-permute-done.1 = bf16[512,256]{1,0:T(8,128)(2,1)S(1)} collective-permute-done((bf16[512,256]{1,0:T(8,128)(2,1)S(1)}, bf16[512,256]{1,0:T(8,128)(2,1)S(1)}, u32[]{:S(2)}, u32[]{:S(2)}) %collective-permute-start.1) | collective-permute-done | bytes 262176 | tf_op jit(solution)/shard_map/while/body/eval_jaxpr/ppermute | solution.py:14
  238.2 6.9 %collective-permute-done.1 = bf16[512,256]{1,0:T(8,128)(2,1)S(1)} collective-permute-done((bf16[512,256]{1,0:T(8,128)(2,1)S(1)}, bf16[512,256]{1,0:T(8,128)(2,1)S(1)}, u32[]{:S(2)}, u32[]{:S(2)}) %collective-permute-start.1) | collective-permute-done | bytes 262176 | tf_op jit(solution)/shard_map/while/body/eval_jaxpr/ppermute | solution.py:14
  247.9 6.6 %collective-permute-done.1 = bf16[512,256]{1,0:T(8,128)(2,1)S(1)} collective-permute-done((bf16[512,256]{1,0:T(8,128)(2,1)S(1)}, bf16[512,256]{1,0:T(8,128)(2,1)S(1)}, u32[]{:S(2)}, u32[]{:S(2)}) %collective-permute-start.1) | collective-permute-done | bytes 262176 | tf_op jit(solution)/shard_map/while/body/eval_jaxpr/ppermute | solution.py:14
  257.3 6.6 %collective-permute-done.1 = bf16[512,256]{1,0:T(8,128)(2,1)S(1)} collective-permute-done((bf16[512,256]{1,0:T(8,128)(2,1)S(1)}, bf16[512,256]{1,0:T(8,128)(2,1)S(1)}, u32[]{:S(2)}, u32[]{:S(2)}) %collective-permute-start.1) | collective-permute-done | bytes 262176 | tf_op jit(solution)/shard_map/while/body/eval_jaxpr/ppermute | solution.py:14
  266.7 6.7 %collective-permute-done.1 = bf16[512,256]{1,0:T(8,128)(2,1)S(1)} collective-permute-done((bf16[512,256]{1,0:T(8,128)(2,1)S(1)}, bf16[512,256]{1,0:T(8,128)(2,1)S(1)}, u32[]{:S(2)}, u32[]{:S(2)}) %collective-permute-start.1) | collective-permute-done | bytes 262176 | tf_op jit(solution)/shard_map/while/body/eval_jaxpr/ppermute | solution.py:14
  276.2 7.8 %collective-permute-done.1 = bf16[512,256]{1,0:T(8,128)(2,1)S(1)} collective-permute-done((bf16[512,256]{1,0:T(8,128)(2,1)S(1)}, bf16[512,256]{1,0:T(8,128)(2,1)S(1)}, u32[]{:S(2)}, u32[]{:S(2)}) %collective-permute-start.1) | collective-permute-done | bytes 262176 | tf_op jit(solution)/shard_map/while/body/eval_jaxpr/ppermute | solution.py:14
  287.5 8.3 %collective-permute-done.1 = bf16[512,256]{1,0:T(8,128)(2,1)S(1)} collective-permute-done((bf16[512,256]{1,0:T(8,128)(2,1)S(1)}, bf16[512,256]{1,0:T(8,128)(2,1)S(1)}, u32[]{:S(2)}, u32[]{:S(2)}) %collective-permute-start.1) | collective-permute-done | bytes 262176 | tf_op jit(solution)/shard_map/while/body/eval_jaxpr/ppermute | solution.py:14
  298.9 8.3 %collective-permute-done.1 = bf16[512,256]{1,0:T(8,128)(2,1)S(1)} collective-permute-done((bf16[512,256]{1,0:T(8,128)(2,1)S(1)}, bf16[512,256]{1,0:T(8,128)(2,1)S(1)}, u32[]{:S(2)}, u32[]{:S(2)}) %collective-permute-start.1) | collective-permute-done | bytes 262176 | tf_op jit(solution)/shard_map/while/body/eval_jaxpr/ppermute | solution.py:14
  311.7 6.2 %collective-permute-done.1 = bf16[512,256]{1,0:T(8,128)(2,1)S(1)} collective-permute-done((bf16[512,256]{1,0:T(8,128)(2,1)S(1)}, bf16[512,256]{1,0:T(8,128)(2,1)S(1)}, u32[]{:S(2)}, u32[]{:S(2)}) %collective-permute-start.1) | collective-permute-done | bytes 262176 | tf_op jit(solution)/shard_map/while/body/eval_jaxpr/ppermute | solution.py:14
  318.6 5.4 %collective-permute-start.1 = (bf16[512,256]{1,0:T(8,128)(2,1)S(1)}, bf16[512,256]{1,0:T(8,128)(2,1)S(1)}, u32[]{:S(2)}, u32[]{:S(2)}) collective-permute-start(bf16[512,256]{1,0:T(8,128)(2,1)S(1)} %get-tuple-element.664), channel_id=1, source_target_pairs={{4,0},{8,4},{12,8},{16,12},{20,16},{24,20},{28,24},{32,28},{36,32}... | collective-permute-start | bytes 786440 | tf_op jit(solution)/shard_map/while/body/eval_jaxpr/ppermute | solution.py:14
  325.9 4.6 %collective-permute-done.1 = bf16[512,256]{1,0:T(8,128)(2,1)S(1)} collective-permute-done((bf16[512,256]{1,0:T(8,128)(2,1)S(1)}, bf16[512,256]{1,0:T(8,128)(2,1)S(1)}, u32[]{:S(2)}, u32[]{:S(2)}) %collective-permute-start.1) | collective-permute-done | bytes 262176 | tf_op jit(solution)/shard_map/while/body/eval_jaxpr/ppermute | solution.py:14
  331.3 7.1 %collective-permute-start.1 = (bf16[512,256]{1,0:T(8,128)(2,1)S(1)}, bf16[512,256]{1,0:T(8,128)(2,1)S(1)}, u32[]{:S(2)}, u32[]{:S(2)}) collective-permute-start(bf16[512,256]{1,0:T(8,128)(2,1)S(1)} %get-tuple-element.664), channel_id=1, source_target_pairs={{4,0},{8,4},{12,8},{16,12},{20,16},{24,20},{28,24},{32,28},{36,32}... | collective-permute-start | bytes 786440 | tf_op jit(solution)/shard_map/while/body/eval_jaxpr/ppermute | solution.py:14
  344.5 6.5 %collective-permute-start.1 = (bf16[512,256]{1,0:T(8,128)(2,1)S(1)}, bf16[512,256]{1,0:T(8,128)(2,1)S(1)}, u32[]{:S(2)}, u32[]{:S(2)}) collective-permute-start(bf16[512,256]{1,0:T(8,128)(2,1)S(1)} %get-tuple-element.664), channel_id=1, source_target_pairs={{4,0},{8,4},{12,8},{16,12},{20,16},{24,20},{28,24},{32,28},{36,32}... | collective-permute-start | bytes 786440 | tf_op jit(solution)/shard_map/while/body/eval_jaxpr/ppermute | solution.py:14
  356.1 6.6 %collective-permute-start.1 = (bf16[512,256]{1,0:T(8,128)(2,1)S(1)}, bf16[512,256]{1,0:T(8,128)(2,1)S(1)}, u32[]{:S(2)}, u32[]{:S(2)}) collective-permute-start(bf16[512,256]{1,0:T(8,128)(2,1)S(1)} %get-tuple-element.664), channel_id=1, source_target_pairs={{4,0},{8,4},{12,8},{16,12},{20,16},{24,20},{28,24},{32,28},{36,32}... | collective-permute-start | bytes 786440 | tf_op jit(solution)/shard_map/while/body/eval_jaxpr/ppermute | solution.py:14
  367.4 6.8 %collective-permute-start.1 = (bf16[512,256]{1,0:T(8,128)(2,1)S(1)}, bf16[512,256]{1,0:T(8,128)(2,1)S(1)}, u32[]{:S(2)}, u32[]{:S(2)}) collective-permute-start(bf16[512,256]{1,0:T(8,128)(2,1)S(1)} %get-tuple-element.664), channel_id=1, source_target_pairs={{4,0},{8,4},{12,8},{16,12},{20,16},{24,20},{28,24},{32,28},{36,32}... | collective-permute-start | bytes 786440 | tf_op jit(solution)/shard_map/while/body/eval_jaxpr/ppermute | solution.py:14
  382.6 28.1 %all-to-all-start.2 = ((bf16[128,12,256]{2,1,0:T(8,128)(2,1)}), bf16[128,12,256]{2,1,0:T(8,128)(2,1)S(1)}, u32[]{:S(2)}, u32[]{:S(2)}) async-start(bf16[128,12,256]{2,1,0:T(8,128)(2,1)} %all_to_all.22), calls=%async_computation.2 | async-start | bytes 2097152 | tf_op jit(solution)/shard_map/all_to_all | solution.py:117
  413.6 14.9 %all-to-all-done.2 = bf16[128,12,256]{2,1,0:T(8,128)(2,1)S(1)} async-done(((bf16[128,12,256]{2,1,0:T(8,128)(2,1)}), bf16[128,12,256]{2,1,0:T(8,128)(2,1)S(1)}, u32[]{:S(2)}, u32[]{:S(2)}) %all-to-all-start.2) | async-done | bytes 786464 | tf_op jit(solution)/shard_map/all_to_all | solution.py:117
  428.7 15.5 %scatter_custom_fusion.2 = f32[16384,256]{1,0:T(8,128)} fusion(s32[1536]{0:T(1024)S(1)} %fusion.30, f32[1536,256]{1,0:T(8,128)S(1)} %reshape.84, f32[]{:T(128)} %constant.196.clone.1), kind=kCustom, calls=%fused_computation.28 | custom fusion | flops 393216 | bytes 16777220 | tf_op jit(solution)/shard_map/scatter-add | solution.py:123
  444.2 8.9 %convert_element_type.71 = bf16[16384,256]{1,0:T(8,128)(2,1)} convert(f32[16384,256]{1,0:T(8,128)} %scatter_custom_fusion.2) | non-fusion elementwise | flops 4194304 | bytes 25165824 | tf_op jit(solution)/shard_map/convert_element_type | solution.py:124
  (219 shorter events, 95.4 us)
Async XLA Ops:
  0.6 4.1 copy-start.2
  0.6 4.1 copy-start
  4.7 194.6 %copy-start.3 = (s32[512]{0:T(512)S(1)}, s32[512]{0:T(512)}, u32[]{:S(2)}) copy-start(s32[512]{0:T(512)} %param.11) | copy-start | bytes 6148
  4.7 195.0 %copy-start.1 = (bf16[512,256]{1,0:T(8,128)(2,1)S(1)}, bf16[512,256]{1,0:T(8,128)(2,1)}, u32[]{:S(2)}) copy-start(bf16[512,256]{1,0:T(8,128)(2,1)} %param.10) | copy-start | bytes 786436
  4.7 195.5 %copy-start.4 = (s32[512,1]{0,1:T(1,128)S(1)}, s32[512,1]{0,1:T(1,128)}, u32[]{:S(2)}) copy-start(s32[512,1]{0,1:T(1,128)} %param.12) | copy-start | bytes 6148
  4.7 8.1 %collective-permute-start = (bf16[512,256]{1,0:T(8,128)(2,1)S(1)}, bf16[512,256]{1,0:T(8,128)(2,1)S(1)}, u32[]{:S(2)}, u32[]{:S(2)}) collective-permute-start(bf16[512,256]{1,0:T(8,128)(2,1)S(1)} %get-tuple-element.629), channel_id=1, source_target_pairs={{124,0},{0,4},{4,8},{8,12},{12,16},{16,20},{20,24},{24,28},{28,32}... | collective-permute-start | bytes 786440 | tf_op jit(solution)/shard_map/while/body/eval_jaxpr/ppermute | solution.py:14
  14.2 8.4 %collective-permute-start = (bf16[512,256]{1,0:T(8,128)(2,1)S(1)}, bf16[512,256]{1,0:T(8,128)(2,1)S(1)}, u32[]{:S(2)}, u32[]{:S(2)}) collective-permute-start(bf16[512,256]{1,0:T(8,128)(2,1)S(1)} %get-tuple-element.629), channel_id=1, source_target_pairs={{124,0},{0,4},{4,8},{8,12},{12,16},{16,20},{20,24},{24,28},{28,32}... | collective-permute-start | bytes 786440 | tf_op jit(solution)/shard_map/while/body/eval_jaxpr/ppermute | solution.py:14
  23.9 8.5 %collective-permute-start = (bf16[512,256]{1,0:T(8,128)(2,1)S(1)}, bf16[512,256]{1,0:T(8,128)(2,1)S(1)}, u32[]{:S(2)}, u32[]{:S(2)}) collective-permute-start(bf16[512,256]{1,0:T(8,128)(2,1)S(1)} %get-tuple-element.629), channel_id=1, source_target_pairs={{124,0},{0,4},{4,8},{8,12},{12,16},{16,20},{20,24},{24,28},{28,32}... | collective-permute-start | bytes 786440 | tf_op jit(solution)/shard_map/while/body/eval_jaxpr/ppermute | solution.py:14
  33.7 8.5 %collective-permute-start = (bf16[512,256]{1,0:T(8,128)(2,1)S(1)}, bf16[512,256]{1,0:T(8,128)(2,1)S(1)}, u32[]{:S(2)}, u32[]{:S(2)}) collective-permute-start(bf16[512,256]{1,0:T(8,128)(2,1)S(1)} %get-tuple-element.629), channel_id=1, source_target_pairs={{124,0},{0,4},{4,8},{8,12},{12,16},{16,20},{20,24},{24,28},{28,32}... | collective-permute-start | bytes 786440 | tf_op jit(solution)/shard_map/while/body/eval_jaxpr/ppermute | solution.py:14
  43.5 8.5 %collective-permute-start = (bf16[512,256]{1,0:T(8,128)(2,1)S(1)}, bf16[512,256]{1,0:T(8,128)(2,1)S(1)}, u32[]{:S(2)}, u32[]{:S(2)}) collective-permute-start(bf16[512,256]{1,0:T(8,128)(2,1)S(1)} %get-tuple-element.629), channel_id=1, source_target_pairs={{124,0},{0,4},{4,8},{8,12},{12,16},{16,20},{20,24},{24,28},{28,32}... | collective-permute-start | bytes 786440 | tf_op jit(solution)/shard_map/while/body/eval_jaxpr/ppermute | solution.py:14
  53.3 8.9 %collective-permute-start = (bf16[512,256]{1,0:T(8,128)(2,1)S(1)}, bf16[512,256]{1,0:T(8,128)(2,1)S(1)}, u32[]{:S(2)}, u32[]{:S(2)}) collective-permute-start(bf16[512,256]{1,0:T(8,128)(2,1)S(1)} %get-tuple-element.629), channel_id=1, source_target_pairs={{124,0},{0,4},{4,8},{8,12},{12,16},{16,20},{20,24},{24,28},{28,32}... | collective-permute-start | bytes 786440 | tf_op jit(solution)/shard_map/while/body/eval_jaxpr/ppermute | solution.py:14
  63.5 10.1 %collective-permute-start = (bf16[512,256]{1,0:T(8,128)(2,1)S(1)}, bf16[512,256]{1,0:T(8,128)(2,1)S(1)}, u32[]{:S(2)}, u32[]{:S(2)}) collective-permute-start(bf16[512,256]{1,0:T(8,128)(2,1)S(1)} %get-tuple-element.629), channel_id=1, source_target_pairs={{124,0},{0,4},{4,8},{8,12},{12,16},{16,20},{20,24},{24,28},{28,32}... | collective-permute-start | bytes 786440 | tf_op jit(solution)/shard_map/while/body/eval_jaxpr/ppermute | solution.py:14
  74.9 11.2 %collective-permute-start = (bf16[512,256]{1,0:T(8,128)(2,1)S(1)}, bf16[512,256]{1,0:T(8,128)(2,1)S(1)}, u32[]{:S(2)}, u32[]{:S(2)}) collective-permute-start(bf16[512,256]{1,0:T(8,128)(2,1)S(1)} %get-tuple-element.629), channel_id=1, source_target_pairs={{124,0},{0,4},{4,8},{8,12},{12,16},{16,20},{20,24},{24,28},{28,32}... | collective-permute-start | bytes 786440 | tf_op jit(solution)/shard_map/while/body/eval_jaxpr/ppermute | solution.py:14
  87.5 10.4 %collective-permute-start = (bf16[512,256]{1,0:T(8,128)(2,1)S(1)}, bf16[512,256]{1,0:T(8,128)(2,1)S(1)}, u32[]{:S(2)}, u32[]{:S(2)}) collective-permute-start(bf16[512,256]{1,0:T(8,128)(2,1)S(1)} %get-tuple-element.629), channel_id=1, source_target_pairs={{124,0},{0,4},{4,8},{8,12},{12,16},{16,20},{20,24},{24,28},{28,32}... | collective-permute-start | bytes 786440 | tf_op jit(solution)/shard_map/while/body/eval_jaxpr/ppermute | solution.py:14
  99.2 12.1 %collective-permute-start = (bf16[512,256]{1,0:T(8,128)(2,1)S(1)}, bf16[512,256]{1,0:T(8,128)(2,1)S(1)}, u32[]{:S(2)}, u32[]{:S(2)}) collective-permute-start(bf16[512,256]{1,0:T(8,128)(2,1)S(1)} %get-tuple-element.629), channel_id=1, source_target_pairs={{124,0},{0,4},{4,8},{8,12},{12,16},{16,20},{20,24},{24,28},{28,32}... | collective-permute-start | bytes 786440 | tf_op jit(solution)/shard_map/while/body/eval_jaxpr/ppermute | solution.py:14
  112.7 13.9 %collective-permute-start = (bf16[512,256]{1,0:T(8,128)(2,1)S(1)}, bf16[512,256]{1,0:T(8,128)(2,1)S(1)}, u32[]{:S(2)}, u32[]{:S(2)}) collective-permute-start(bf16[512,256]{1,0:T(8,128)(2,1)S(1)} %get-tuple-element.629), channel_id=1, source_target_pairs={{124,0},{0,4},{4,8},{8,12},{12,16},{16,20},{20,24},{24,28},{28,32}... | collective-permute-start | bytes 786440 | tf_op jit(solution)/shard_map/while/body/eval_jaxpr/ppermute | solution.py:14
  127.9 13.2 %collective-permute-start = (bf16[512,256]{1,0:T(8,128)(2,1)S(1)}, bf16[512,256]{1,0:T(8,128)(2,1)S(1)}, u32[]{:S(2)}, u32[]{:S(2)}) collective-permute-start(bf16[512,256]{1,0:T(8,128)(2,1)S(1)} %get-tuple-element.629), channel_id=1, source_target_pairs={{124,0},{0,4},{4,8},{8,12},{12,16},{16,20},{20,24},{24,28},{28,32}... | collective-permute-start | bytes 786440 | tf_op jit(solution)/shard_map/while/body/eval_jaxpr/ppermute | solution.py:14
  142.4 11.5 %collective-permute-start = (bf16[512,256]{1,0:T(8,128)(2,1)S(1)}, bf16[512,256]{1,0:T(8,128)(2,1)S(1)}, u32[]{:S(2)}, u32[]{:S(2)}) collective-permute-start(bf16[512,256]{1,0:T(8,128)(2,1)S(1)} %get-tuple-element.629), channel_id=1, source_target_pairs={{124,0},{0,4},{4,8},{8,12},{12,16},{16,20},{20,24},{24,28},{28,32}... | collective-permute-start | bytes 786440 | tf_op jit(solution)/shard_map/while/body/eval_jaxpr/ppermute | solution.py:14
  155.3 10.1 %collective-permute-start = (bf16[512,256]{1,0:T(8,128)(2,1)S(1)}, bf16[512,256]{1,0:T(8,128)(2,1)S(1)}, u32[]{:S(2)}, u32[]{:S(2)}) collective-permute-start(bf16[512,256]{1,0:T(8,128)(2,1)S(1)} %get-tuple-element.629), channel_id=1, source_target_pairs={{124,0},{0,4},{4,8},{8,12},{12,16},{16,20},{20,24},{24,28},{28,32}... | collective-permute-start | bytes 786440 | tf_op jit(solution)/shard_map/while/body/eval_jaxpr/ppermute | solution.py:14
  166.7 9.8 %collective-permute-start = (bf16[512,256]{1,0:T(8,128)(2,1)S(1)}, bf16[512,256]{1,0:T(8,128)(2,1)S(1)}, u32[]{:S(2)}, u32[]{:S(2)}) collective-permute-start(bf16[512,256]{1,0:T(8,128)(2,1)S(1)} %get-tuple-element.629), channel_id=1, source_target_pairs={{124,0},{0,4},{4,8},{8,12},{12,16},{16,20},{20,24},{24,28},{28,32}... | collective-permute-start | bytes 786440 | tf_op jit(solution)/shard_map/while/body/eval_jaxpr/ppermute | solution.py:14
  178.5 27.4 %all-to-all-start = ((f32[32,1,512]{2,1,0:T(1,128)}), f32[32,1,512]{2,1,0:T(1,128)S(1)}, u32[]{:S(2)}, u32[]{:S(2)}) async-start(f32[32,1,512]{2,1,0:T(1,128)} %broadcast_in_dim.43), calls=%async_computation | async-start | bytes 131072 | tf_op jit(solution)/shard_map/all_to_all | solution.py:19
  205.9 176.7 %all-to-all-start.1 = ((s32[128,12,1]{1,2,0:T(1,128)}), s32[128,12,1]{1,2,0:T(1,128)S(1)}, u32[]{:S(2)}, u32[]{:S(2)}) async-start(s32[128,12,1]{1,2,0:T(1,128)} %bitcast.6), calls=%async_computation.1 | async-start | bytes 131072 | tf_op jit(solution)/shard_map/all_to_all | solution.py:118
  214.0 10.8 %collective-permute-start.1 = (bf16[512,256]{1,0:T(8,128)(2,1)S(1)}, bf16[512,256]{1,0:T(8,128)(2,1)S(1)}, u32[]{:S(2)}, u32[]{:S(2)}) collective-permute-start(bf16[512,256]{1,0:T(8,128)(2,1)S(1)} %get-tuple-element.664), channel_id=1, source_target_pairs={{4,0},{8,4},{12,8},{16,12},{20,16},{24,20},{28,24},{32,28},{36,32}... | collective-permute-start | bytes 786440 | tf_op jit(solution)/shard_map/while/body/eval_jaxpr/ppermute | solution.py:14
  225.5 9.8 %collective-permute-start.1 = (bf16[512,256]{1,0:T(8,128)(2,1)S(1)}, bf16[512,256]{1,0:T(8,128)(2,1)S(1)}, u32[]{:S(2)}, u32[]{:S(2)}) collective-permute-start(bf16[512,256]{1,0:T(8,128)(2,1)S(1)} %get-tuple-element.664), channel_id=1, source_target_pairs={{4,0},{8,4},{12,8},{16,12},{20,16},{24,20},{28,24},{32,28},{36,32}... | collective-permute-start | bytes 786440 | tf_op jit(solution)/shard_map/while/body/eval_jaxpr/ppermute | solution.py:14
  236.2 9.0 %collective-permute-start.1 = (bf16[512,256]{1,0:T(8,128)(2,1)S(1)}, bf16[512,256]{1,0:T(8,128)(2,1)S(1)}, u32[]{:S(2)}, u32[]{:S(2)}) collective-permute-start(bf16[512,256]{1,0:T(8,128)(2,1)S(1)} %get-tuple-element.664), channel_id=1, source_target_pairs={{4,0},{8,4},{12,8},{16,12},{20,16},{24,20},{28,24},{32,28},{36,32}... | collective-permute-start | bytes 786440 | tf_op jit(solution)/shard_map/while/body/eval_jaxpr/ppermute | solution.py:14
  246.0 8.6 %collective-permute-start.1 = (bf16[512,256]{1,0:T(8,128)(2,1)S(1)}, bf16[512,256]{1,0:T(8,128)(2,1)S(1)}, u32[]{:S(2)}, u32[]{:S(2)}) collective-permute-start(bf16[512,256]{1,0:T(8,128)(2,1)S(1)} %get-tuple-element.664), channel_id=1, source_target_pairs={{4,0},{8,4},{12,8},{16,12},{20,16},{24,20},{28,24},{32,28},{36,32}... | collective-permute-start | bytes 786440 | tf_op jit(solution)/shard_map/while/body/eval_jaxpr/ppermute | solution.py:14
  255.3 8.6 %collective-permute-start.1 = (bf16[512,256]{1,0:T(8,128)(2,1)S(1)}, bf16[512,256]{1,0:T(8,128)(2,1)S(1)}, u32[]{:S(2)}, u32[]{:S(2)}) collective-permute-start(bf16[512,256]{1,0:T(8,128)(2,1)S(1)} %get-tuple-element.664), channel_id=1, source_target_pairs={{4,0},{8,4},{12,8},{16,12},{20,16},{24,20},{28,24},{32,28},{36,32}... | collective-permute-start | bytes 786440 | tf_op jit(solution)/shard_map/while/body/eval_jaxpr/ppermute | solution.py:14
  264.7 8.7 %collective-permute-start.1 = (bf16[512,256]{1,0:T(8,128)(2,1)S(1)}, bf16[512,256]{1,0:T(8,128)(2,1)S(1)}, u32[]{:S(2)}, u32[]{:S(2)}) collective-permute-start(bf16[512,256]{1,0:T(8,128)(2,1)S(1)} %get-tuple-element.664), channel_id=1, source_target_pairs={{4,0},{8,4},{12,8},{16,12},{20,16},{24,20},{28,24},{32,28},{36,32}... | collective-permute-start | bytes 786440 | tf_op jit(solution)/shard_map/while/body/eval_jaxpr/ppermute | solution.py:14
  274.2 9.8 %collective-permute-start.1 = (bf16[512,256]{1,0:T(8,128)(2,1)S(1)}, bf16[512,256]{1,0:T(8,128)(2,1)S(1)}, u32[]{:S(2)}, u32[]{:S(2)}) collective-permute-start(bf16[512,256]{1,0:T(8,128)(2,1)S(1)} %get-tuple-element.664), channel_id=1, source_target_pairs={{4,0},{8,4},{12,8},{16,12},{20,16},{24,20},{28,24},{32,28},{36,32}... | collective-permute-start | bytes 786440 | tf_op jit(solution)/shard_map/while/body/eval_jaxpr/ppermute | solution.py:14
  284.9 11.0 %collective-permute-start.1 = (bf16[512,256]{1,0:T(8,128)(2,1)S(1)}, bf16[512,256]{1,0:T(8,128)(2,1)S(1)}, u32[]{:S(2)}, u32[]{:S(2)}) collective-permute-start(bf16[512,256]{1,0:T(8,128)(2,1)S(1)} %get-tuple-element.664), channel_id=1, source_target_pairs={{4,0},{8,4},{12,8},{16,12},{20,16},{24,20},{28,24},{32,28},{36,32}... | collective-permute-start | bytes 786440 | tf_op jit(solution)/shard_map/while/body/eval_jaxpr/ppermute | solution.py:14
  296.7 10.6 %collective-permute-start.1 = (bf16[512,256]{1,0:T(8,128)(2,1)S(1)}, bf16[512,256]{1,0:T(8,128)(2,1)S(1)}, u32[]{:S(2)}, u32[]{:S(2)}) collective-permute-start(bf16[512,256]{1,0:T(8,128)(2,1)S(1)} %get-tuple-element.664), channel_id=1, source_target_pairs={{4,0},{8,4},{12,8},{16,12},{20,16},{24,20},{28,24},{32,28},{36,32}... | collective-permute-start | bytes 786440 | tf_op jit(solution)/shard_map/while/body/eval_jaxpr/ppermute | solution.py:14
  308.1 9.7 %collective-permute-start.1 = (bf16[512,256]{1,0:T(8,128)(2,1)S(1)}, bf16[512,256]{1,0:T(8,128)(2,1)S(1)}, u32[]{:S(2)}, u32[]{:S(2)}) collective-permute-start(bf16[512,256]{1,0:T(8,128)(2,1)S(1)} %get-tuple-element.664), channel_id=1, source_target_pairs={{4,0},{8,4},{12,8},{16,12},{20,16},{24,20},{28,24},{32,28},{36,32}... | collective-permute-start | bytes 786440 | tf_op jit(solution)/shard_map/while/body/eval_jaxpr/ppermute | solution.py:14
  318.6 11.9 %collective-permute-start.1 = (bf16[512,256]{1,0:T(8,128)(2,1)S(1)}, bf16[512,256]{1,0:T(8,128)(2,1)S(1)}, u32[]{:S(2)}, u32[]{:S(2)}) collective-permute-start(bf16[512,256]{1,0:T(8,128)(2,1)S(1)} %get-tuple-element.664), channel_id=1, source_target_pairs={{4,0},{8,4},{12,8},{16,12},{20,16},{24,20},{28,24},{32,28},{36,32}... | collective-permute-start | bytes 786440 | tf_op jit(solution)/shard_map/while/body/eval_jaxpr/ppermute | solution.py:14
  331.3 12.4 %collective-permute-start.1 = (bf16[512,256]{1,0:T(8,128)(2,1)S(1)}, bf16[512,256]{1,0:T(8,128)(2,1)S(1)}, u32[]{:S(2)}, u32[]{:S(2)}) collective-permute-start(bf16[512,256]{1,0:T(8,128)(2,1)S(1)} %get-tuple-element.664), channel_id=1, source_target_pairs={{4,0},{8,4},{12,8},{16,12},{20,16},{24,20},{28,24},{32,28},{36,32}... | collective-permute-start | bytes 786440 | tf_op jit(solution)/shard_map/while/body/eval_jaxpr/ppermute | solution.py:14
  344.5 10.7 %collective-permute-start.1 = (bf16[512,256]{1,0:T(8,128)(2,1)S(1)}, bf16[512,256]{1,0:T(8,128)(2,1)S(1)}, u32[]{:S(2)}, u32[]{:S(2)}) collective-permute-start(bf16[512,256]{1,0:T(8,128)(2,1)S(1)} %get-tuple-element.664), channel_id=1, source_target_pairs={{4,0},{8,4},{12,8},{16,12},{20,16},{24,20},{28,24},{32,28},{36,32}... | collective-permute-start | bytes 786440 | tf_op jit(solution)/shard_map/while/body/eval_jaxpr/ppermute | solution.py:14
  356.1 10.5 %collective-permute-start.1 = (bf16[512,256]{1,0:T(8,128)(2,1)S(1)}, bf16[512,256]{1,0:T(8,128)(2,1)S(1)}, u32[]{:S(2)}, u32[]{:S(2)}) collective-permute-start(bf16[512,256]{1,0:T(8,128)(2,1)S(1)} %get-tuple-element.664), channel_id=1, source_target_pairs={{4,0},{8,4},{12,8},{16,12},{20,16},{24,20},{28,24},{32,28},{36,32}... | collective-permute-start | bytes 786440 | tf_op jit(solution)/shard_map/while/body/eval_jaxpr/ppermute | solution.py:14
  367.4 10.7 %collective-permute-start.1 = (bf16[512,256]{1,0:T(8,128)(2,1)S(1)}, bf16[512,256]{1,0:T(8,128)(2,1)S(1)}, u32[]{:S(2)}, u32[]{:S(2)}) collective-permute-start(bf16[512,256]{1,0:T(8,128)(2,1)S(1)} %get-tuple-element.664), channel_id=1, source_target_pairs={{4,0},{8,4},{12,8},{16,12},{20,16},{24,20},{28,24},{32,28},{36,32}... | collective-permute-start | bytes 786440 | tf_op jit(solution)/shard_map/while/body/eval_jaxpr/ppermute | solution.py:14
  382.6 45.9 %all-to-all-start.2 = ((bf16[128,12,256]{2,1,0:T(8,128)(2,1)}), bf16[128,12,256]{2,1,0:T(8,128)(2,1)S(1)}, u32[]{:S(2)}, u32[]{:S(2)}) async-start(bf16[128,12,256]{2,1,0:T(8,128)(2,1)} %all_to_all.22), calls=%async_computation.2 | async-start | bytes 2097152 | tf_op jit(solution)/shard_map/all_to_all | solution.py:117
where the time goes:
time: 456 us; the launch traced here: 453 us
  waiting for transfers between devices  214 us (47%)
  starting transfers between devices  138 us (30%)
  matrix products  46.4 us (10%)
  other arithmetic  32.8 us (7%)
  local copies, waits for them, and re-layouts  21 us (5%)
    ppermute x30, waiting for transfers between devices, passed_along(): return lax.ppermute(block, axis, route)  197 us
    ppermute x30, starting transfers between devices, passed_along(): return lax.ppermute(block, axis, route)  80.6 us
    all_to_all x1, starting transfers between devices, local(): lax.all_to_all(send_rows, ('blk', 'table'), split_axis=0, concat_axis=0,...  28.1 us
    dot_general x15, matrix products, backward(): jnp.dot(weights, item_block, preferred_element_type=jnp.float32)  27 us
    all_to_all x1, starting transfers between devices, from_everyone(): return lax.all_to_all(copies, axis, split_axis=0, concat_axis=0, tiled=True)  20.8 us
    scatter-add x1, other arithmetic, local(): table_grad = jnp.zeros((ROWS_DEV, feature_width), jnp.float32).at[got_ids...  15.5 us
    all_to_all x1, waiting for transfers between devices, local(): lax.all_to_all(send_rows, ('blk', 'table'), split_axis=0, concat_axis=0,...  14.9 us
    dot_general x15, matrix products, backward(): lax.dot_general(their_weights, query_block, (((0,), (0,)), ((), ())), pre...  11.7 us
  transfers between devices with their start and end apart: 33, of which 32 were waited for; matrix products, arithmetic and copies ran while one was open for 11% of the time, Pallas kernels for 0%

commit v1 on v0

v1 whole, which is shorter than its diff:
```python
import math

import jax
import jax.numpy as jnp
from jax import lax
from jax.experimental import pallas as pl
from jax.experimental.pallas import tpu as pltpu
from jax.sharding import PartitionSpec as P

ROWS_DEV = 16384
N = 512
D = 256
H = 256
SCALE = 3.0 / math.sqrt(D)
LOG2E = 1.4426950408889634
C2 = SCALE * LOG2E
MESH = pl.DeviceIdType.MESH
NT = (((1,), (1,)), ((), ()))
NN = (((1,), (0,)), ((), ()))
F32 = jnp.float32
BF16 = jnp.bfloat16


def main_kernel(
    q_hbm, k_hbm, pos_ref,
    dq_ref, dk_ref,
    qbuf, kbuf, sbuf, gbuf, kt, lk, lst, lse, acc, pk, pr, dqs, dqr,
    lsem, ssem, rsem, st_s, st_r, dq_s, dq_r,
):
    b = lax.axis_index("blk")
    x = b // 8
    me = b % 8
    z = me // 4
    y = me % 4

    def slot(r, s):
        return 4 * ((z + s) % 2) + (y + r) % 4

    def group(p):
        return {"blk": x * 8 + p}

    xp = {"blk": ((x + 1) % 4) * 8 + me}
    xm = {"blk": ((x + 3) % 4) * 8 + me}
    yp = group(slot(1, 0))
    ym = group(slot(3, 0))
    zp = group(slot(0, 1))

    own_q = pltpu.make_async_copy(q_hbm, qbuf.at[me], lsem.at[0])
    own_k = pltpu.make_async_copy(k_hbm, kbuf.at[0], lsem.at[1])
    own_q.start()
    own_k.start()

    barrier = pltpu.get_barrier_semaphore()
    for o in range(1, 8):
        pl.semaphore_signal(barrier, inc=1, device_id=group((me + o) % 8), device_id_type=MESH)
    for dev in (xp, xm):
        pl.semaphore_signal(barrier, inc=1, device_id=dev, device_id_type=MESH)
    pl.semaphore_wait(barrier, 9)
    own_k.wait()
    own_q.wait()

    def half(ref, i, c):
        return ref.at[i, pl.ds(c * H, H)]

    def send(n, src, dst, dev):
        copy = pltpu.make_async_remote_copy(
            src_ref=src, dst_ref=dst, send_sem=ssem.at[n], recv_sem=rsem.at[n],
            device_id=dev, device_id_type=MESH,
        )
        copy.start()
        return copy

    def arrived(n, ref):
        pltpu.make_async_remote_copy(
            src_ref=ref, dst_ref=ref, send_sem=ssem.at[n], recv_sem=rsem.at[n],
            device_id=xp, device_id_type=MESH,
        ).wait_recv()

    sent = []

    def k_send(n, i, j, c):
        sent.append(send(n, half(kbuf, i, c), half(kbuf, j, c), xp))

    def q_send(n, i, c, dev):
        sent.append(send(n, half(qbuf, i, c), half(qbuf, i, c), dev))

    k_send(0, 0, 1, 0)
    q_send(4, me, 0, yp)
    q_send(7, me, 1, ym)
    q_send(8, me, 0, zp)
    k_send(1, 0, 1, 1)
    q_send(5, me, 1, yp)
    q_send(6, me, 0, ym)
    q_send(9, me, 1, zp)

    def scores(qi, kind, ks):
        q = qbuf[qi]

        def tile(t, top):
            s = lax.dot_general(kbuf[ks, pl.ds(t * H, H), :], q, NT, preferred_element_type=F32)
            sbuf[kind, qi, pl.ds(t * H, H), :] = s
            return jnp.maximum(top, jnp.max(s.reshape(H // 8, 8, N), axis=0))

        top = lax.fori_loop(0, 2, tile, jnp.full((8, N), -jnp.inf, F32))
        top = jnp.max(top, axis=0, keepdims=True) * C2

        def tile2(t, total):
            s = sbuf[kind, qi, pl.ds(t * H, H), :]
            return total + jnp.sum(jnp.exp2(s * C2 - top).reshape(H // 8, 8, N), axis=0)

        total = lax.fori_loop(0, 2, tile2, jnp.zeros((8, N), F32))
        total = jnp.sum(total, axis=0, keepdims=True)
        lk[kind, pl.ds(qi, 1), :] = top + jnp.log(total) * LOG2E

    def mixed_k(qi):
        return jnp.where(qi >= me, 0, 2)

    scores(me, 1, 0)

    s3, s1, s2, s0 = slot(3, 0), slot(1, 0), slot(2, 0), slot(0, 1)
    t3, t1, t2 = slot(3, 1), slot(1, 1), slot(2, 1)
    arrived(0, half(kbuf, 1, 0))
    k_send(2, 1, 2, 0)
    arrived(4, half(qbuf, s3, 0))
    q_send(10, s3, 0, yp)
    arrived(7, half(qbuf, s1, 1))
    q_send(11, s1, 1, ym)
    arrived(8, half(qbuf, s0, 0))
    q_send(12, s0, 0, yp)
    q_send(14, s0, 0, ym)
    arrived(1, half(kbuf, 1, 1))
    k_send(3, 1, 2, 1)
    arrived(9, half(qbuf, s0, 1))
    q_send(13, s0, 1, yp)
    q_send(15, s0, 1, ym)
    arrived(5, half(qbuf, s3, 1))
    arrived(6, half(qbuf, s1, 0))
    scores(me, 0, 1)
    arrived(10, half(qbuf, s2, 0))
    q_send(16, s2, 0, zp)
    arrived(11, half(qbuf, s2, 1))
    q_send(17, s2, 1, zp)

    def first_full(j, carry):
        scores(slot(j, (4 - j) // 4), 0, 1)
        return carry

    lax.fori_loop(0, 4, first_full, 0)
    arrived(2, half(kbuf, 2, 0))
    arrived(3, half(kbuf, 2, 1))

    def turn(i, carry):
        kt[i] = kbuf[i].T
        return carry

    lax.fori_loop(0, 3, turn, 0)

    def first_mixed(j, carry):
        qi = slot(j, (4 - j) // 4)
        scores(qi, 1, mixed_k(qi))
        return carry

    lax.fori_loop(0, 4, first_mixed, 0)
    arrived(12, half(qbuf, t3, 0))
    arrived(14, half(qbuf, t1, 0))
    arrived(13, half(qbuf, t3, 1))
    arrived(15, half(qbuf, t1, 1))
    arrived(16, half(qbuf, t2, 0))
    arrived(17, half(qbuf, t2, 1))

    def last_pairs(j, carry):
        qi = slot(j, 1)
        scores(qi, 0, 1)
        scores(qi, 1, mixed_k(qi))
        return carry

    lax.fori_loop(1, 4, last_pairs, 0)

    a, c = lk[0], lk[1]
    top = jnp.maximum(a, c)
    lst[me] = top + jnp.log(jnp.exp2(a - top) + jnp.exp2(c - top)) * LOG2E
    stats = []
    for o in range(1, 8):
        copy = pltpu.make_async_remote_copy(
            src_ref=lst.at[me], dst_ref=lst.at[me], send_sem=st_s.at[o - 1], recv_sem=st_r.at[o - 1],
            device_id=group((me + o) % 8), device_id_type=MESH,
        )
        copy.start()
        stats.append(copy)
    for o in range(1, 8):
        p = (me + 8 - o) % 8
        pltpu.make_async_remote_copy(
            src_ref=lst.at[p], dst_ref=lst.at[p], send_sem=st_s.at[o - 1], recv_sem=st_r.at[o - 1],
            device_id=xp, device_id_type=MESH,
        ).wait_recv()
    top = lst[0]
    for i in range(1, 8):
        top = jnp.maximum(top, lst[i])
    total = jnp.exp2(lst[0] - top)
    for i in range(1, 8):
        total = total + jnp.exp2(lst[i] - top)
    lse[...] = top + jnp.log(total) * LOG2E

    def item_rows(kind, qi, t, hot):
        w = jnp.exp2(sbuf[kind, qi, pl.ds(t * H, H), :] * C2 - lse[pl.ds(qi, 1), :])
        if hot:
            places = lax.broadcasted_iota(jnp.int32, (H, N), 0) + t * H
            w = jnp.where(places == pos_ref[...], w - 1.0, w)
        w = w.astype(BF16)
        gbuf[kind, qi, pl.ds(t * H, H), :] = w
        acc[pl.ds(t * H, H), :] += jnp.dot(w, qbuf[qi], preferred_element_type=F32)

    def items_of(kind, lo, hi, t, fresh=True):
        if fresh:
            acc[pl.ds(t * H, H), :] = jnp.zeros((H, D), F32)

        def one(qi, carry):
            item_rows(kind, qi, t, False)
            return carry

        lax.fori_loop(lo, hi, one, 0)

    for t in range(2):
        rows = pl.ds(t * H, H)
        items_of(1, 0, me, t)
        pk[0, rows, :] = acc[rows, :].astype(BF16)
        sent.append(send(18 + t, half(pk, 0, t), half(pr, 0, t), xm))
    for t in range(2):
        items_of(0, 0, 8, t)
    for t in range(2):
        rows = pl.ds(t * H, H)
        arrived(18 + t, half(pr, 0, t))
        pk[1, rows, :] = (acc[rows, :] + pr[0, rows, :].astype(F32)).astype(BF16)
        sent.append(send(20 + t, half(pk, 1, t), half(pr, 1, t), xm))
    for t in range(2):
        items_of(1, me + 1, 8, t)
        item_rows(1, me, t, True)

    def query_part(qi):
        ks = mixed_k(qi)
        part = jnp.dot(kt[1], gbuf[0, qi], preferred_element_type=F32)
        return part + jnp.dot(kt[ks], gbuf[1, qi], preferred_element_type=F32)

    def give(o, carry):
        p = (me + o) % 8
        dqs[o] = query_part(p).astype(BF16)
        pltpu.make_async_remote_copy(
            src_ref=dqs.at[o], dst_ref=dqr.at[o], send_sem=dq_s.at[o], recv_sem=dq_r.at[o],
            device_id=group(p), device_id_type=MESH,
        ).start()
        return carry

    lax.fori_loop(1, 8, give, 0)

    for t in range(2):
        rows = pl.ds(t * H, H)
        arrived(20 + t, half(pr, 1, t))
        dk_ref[rows, :] = (SCALE * (acc[rows, :] + pr[1, rows, :].astype(F32))).astype(BF16)

    total = query_part(me)
    for o in range(1, 8):
        pltpu.make_async_remote_copy(
            src_ref=dqs.at[o], dst_ref=dqr.at[o], send_sem=dq_s.at[o], recv_sem=dq_r.at[o],
            device_id=xp, device_id_type=MESH,
        ).wait()
        total = total + dqr[o].astype(F32)
    dq_ref[...] = (SCALE * total).T.astype(BF16)

    for copy in sent:
        copy.wait_send()
    for copy in stats:
        copy.wait_send()


def main_call(queries, items, positives):
    vmem = pl.BlockSpec(memory_space=pltpu.VMEM)
    hbm = pl.BlockSpec(memory_space=pl.ANY)
    dma = pltpu.SemaphoreType.DMA
    return pl.pallas_call(
        main_kernel,
        out_shape=(jax.ShapeDtypeStruct((N, D), BF16), jax.ShapeDtypeStruct((N, D), BF16)),
        in_specs=[hbm, hbm, vmem],
        out_specs=(vmem, vmem),
        scratch_shapes=[
            pltpu.VMEM((8, N, D), BF16),
            pltpu.VMEM((3, N, D), BF16),
            pltpu.VMEM((2, 8, N, N), F32),
            pltpu.VMEM((2, 8, N, N), BF16),
            pltpu.VMEM((3, D, N), BF16),
            pltpu.VMEM((2, 8, N), F32),
            pltpu.VMEM((8, 8, N), F32),
            pltpu.VMEM((8, N), F32),
            pltpu.VMEM((N, D), F32),
            pltpu.VMEM((2, N, D), BF16),
            pltpu.VMEM((2, N, D), BF16),
            pltpu.VMEM((8, D, N), BF16),
            pltpu.VMEM((8, D, N), BF16),
            dma((2,)), dma((22,)), dma((22,)), dma((7,)), dma((7,)), dma((8,)), dma((8,)),
        ],
        compiler_params=pltpu.CompilerParams(
            collective_id=0, has_side_effects=True, vmem_limit_bytes=60 * 1024 * 1024
        ),
        name="band",
    )(queries, items, positives.reshape(1, N))


def local(queries, items, positives, item_owner, item_row):
    size_rows, feature_width = queries.shape
    devices = lax.axis_size("blk") * lax.axis_size("table")
    capacity = 3 * size_rows // devices
    places = jnp.arange(size_rows, dtype=jnp.int32)
    query_grad, item_grad = main_call(queries, items, positives)
    owners = item_owner[:, 0]
    owner_hot = (owners[:, None] == jnp.arange(devices, dtype=jnp.int32)[None, :]).astype(F32)
    earlier = (places[:, None] > places[None, :]).astype(F32)
    before = jnp.dot(earlier, owner_hot, precision=lax.Precision.HIGHEST)
    ranks = jnp.sum(before * owner_hot, axis=1).astype(jnp.int32)
    slots = owners * capacity + ranks
    send_rows = jnp.zeros((devices * capacity, feature_width), BF16).at[slots].set(item_grad)
    send_ids = jnp.full((devices * capacity,), ROWS_DEV, jnp.int32).at[slots].set(item_row)
    got_rows, got_ids = (
        lax.all_to_all(send_rows, ("blk", "table"), split_axis=0, concat_axis=0, tiled=True),
        lax.all_to_all(send_ids, ("blk", "table"), split_axis=0, concat_axis=0, tiled=True),
    )
    table_grad = (
        jnp.zeros((ROWS_DEV, feature_width), F32)
        .at[got_ids]
        .add(got_rows.astype(F32), mode="drop")
        .astype(BF16)
    )
    return (query_grad, item_grad, table_grad)


def solution(mesh):
    in_specs = (
        P(("blk", "table"), None),
        P(("blk", "table"), None),
        P(("blk", "table")),
        P(("blk", "table"), None),
        P(("blk", "table")),
    )
    out_specs = (P(("blk", "table"), None), P(("blk", "table"), None), P(("blk", "table"), None))
    return jax.shard_map(local, mesh=mesh, in_specs=in_specs, out_specs=out_specs, check_vma=False)
```

time: 456 us -> 141 us (0.31)
  waiting for transfers between devices: 214 us -> 16.4 us
  starting transfers between devices: 138 us -> 18.6 us
  Pallas kernels: 0 us -> 66.3 us
  matrix products: 46.4 us -> 1.07 us
  local copies, waits for them, and re-layouts: 21 us -> 9.66 us
  other arithmetic: 32.8 us -> 26.1 us
    ppermute x30 -> x0, waiting for transfers between devices: 197 us -> none  [passed_along(): return lax.ppermute(block, axis, route)]
    ppermute x30 -> x0, starting transfers between devices: 80.6 us -> none  [passed_along(): return lax.ppermute(block, axis, route)]
    pallas_call x0 -> x1, Pallas kernels: none -> 66.3 us  [main_call(): pl.pallas_call(main_kernel, out_shape=(jax.ShapeDtypeStruct((N, D), BF16)...]
    dot_general x48 -> x0, matrix products: 46.1 us -> none  [the longest x15 27 us: backward(): jnp.dot(weights, item_block, preferred_element_type=jnp.float32)]
    all_to_all x1 -> x0, starting transfers between devices: 20.8 us -> none  [from_everyone(): return lax.all_to_all(copies, axis, split_axis=0, concat_axis=0, tiled=True)]
    all_to_all x1, starting transfers between devices: 28.1 us -> 8.34 us  [local(): lax.all_to_all(send_rows, ('blk', 'table'), split_axis=0, concat_axis=0,...]
    dynamic_update_slice x15 -> x0, local copies, waits for them, and re-layouts: 10.9 us -> none  [forward(): lax.dynamic_update_index_in_dim(kept_blocks, item_block, offset, 0)]
    convert_element_type x3 -> x1, other arithmetic: 10.4 us -> 9.02 us  [local(): table_grad = jnp.zeros((ROWS_DEV, feature_width), F32).at[got_ids].add(go...]
  transfers between devices with their start and end apart: 33 -> 2, of which waited for: 32 -> 1; matrix products, arithmetic and copies ran while one was open for 11% -> 3% of each run, Pallas kernels for 0% -> 48%
where the time goes in v1:
time: 141 us; the launch traced here: 139 us
  Pallas kernels  66.3 us (47%)
  other arithmetic  26.1 us (19%)
  starting transfers between devices  18.6 us (13%)
  waiting for transfers between devices  16.4 us (12%)
  local copies, waits for them, and re-layouts  9.66 us (7%)
    pallas_call x1, Pallas kernels, main_call(): pl.pallas_call(main_kernel, out_shape=(jax.ShapeDtypeStruct((N, D), BF16)...  66.3 us
    all_to_all x1, waiting for transfers between devices, local(): lax.all_to_all(send_rows, ('blk', 'table'), split_axis=0, concat_axis=0,...  16.4 us
    scatter-add x1, other arithmetic, local(): table_grad = jnp.zeros((ROWS_DEV, feature_width), F32).at[got_ids].add(go...  15.5 us
    all_to_all x1, starting transfers between devices, local(): lax.all_to_all(send_ids, ('blk', 'table'), split_axis=0, concat_axis=0, t...  10.3 us
    convert_element_type x1, other arithmetic, local(): table_grad = jnp.zeros((ROWS_DEV, feature_width), F32).at[got_ids].add(go...  9.02 us
    all_to_all x1, starting transfers between devices, local(): lax.all_to_all(send_rows, ('blk', 'table'), split_axis=0, concat_axis=0,...  8.34 us
    scatter x1, local copies, waits for them, and re-layouts, local(): jnp.zeros((devices * capacity, feature_width), BF16).at[slots]  2.99 us
  transfers between devices with their start and end apart: 2, of which 1 were waited for; matrix products, arithmetic and copies ran while one was open for 3% of the time, Pallas kernels for 48%

profile of v1, /device:TPU:24, one launch (start us, length us, event | category | flops | bytes accessed | tf_op | source)
XLA Modules:
  0.0 138.8 jit_solution(1264594412116279958)
XLA Ops:
  0.6 1.1 fusion.2
  1.7 0.7 compare_select_fusion.1
  2.4 2.6 %scatter_custom_fusion = s32[1536]{0:T(1024)S(1)} fusion(s32[512]{0:T(512)S(1)} %bitcast.11, s32[512]{0:T(512)} %param.9, s32[]{:T(128)} %constant.7.clone.1), kind=kCustom, calls=%fused_computation.15 | custom fusion | bytes 6656 | tf_op jit(solution)/shard_map/scatter | solution.py:320
  5.0 0.7 all_to_all.14
  5.7 10.3 %all-to-all-start = ((s32[128,12,1]{1,2,0:T(1,128)}), s32[128,12,1]{1,2,0:T(1,128)S(1)}, u32[]{:S(2)}, u32[]{:S(2)}) async-start(s32[128,12,1]{1,2,0:T(1,128)} %bitcast.4), calls=%async_computation | async-start | bytes 131072 | tf_op jit(solution)/shard_map/all_to_all | solution.py:323
  16.0 66.3 %band.1 = (bf16[512,256]{1,0:T(8,128)(2,1)}, bf16[512,256]{1,0:T(8,128)(2,1)}) custom-call(bf16[512,256]{1,0:T(8,128)(2,1)} %q_hbm.1, bf16[512,256]{1,0:T(8,128)(2,1)} %k_hbm.1, s32[1,512]{1,0:T(1,128)} %bitcast.9), custom_call_target="tpu_custom_call" | custom-call | tf_op jit(solution)/shard_map/band/pallas_call | solution.py:279
  82.3 3.0 %scatter_custom_fusion.1 = bf16[1536,256]{1,0:T(8,128)(2,1)S(1)} fusion(s32[512]{0:T(512)S(1)} %bitcast.12, bf16[512,256]{1,0:T(8,128)(2,1)} %get-tuple-element.11, bf16[]{:T(256)} %constant.4.clone.1), kind=kCustom, calls=%fused_computation.8 | custom fusion | bytes 786944 | tf_op jit(solution)/shard_map/scatter | solution.py:319
  85.3 1.1 all_to_all.17
  86.5 0.0 all-to-all-done
  86.5 8.3 %all-to-all-start.1 = ((bf16[128,12,256]{2,1,0:T(8,128)(2,1)}), bf16[128,12,256]{2,1,0:T(8,128)(2,1)S(1)}, u32[]{:S(2)}, u32[]{:S(2)}) async-start(bf16[128,12,256]{2,1,0:T(8,128)(2,1)} %all_to_all.17), calls=%async_computation.1 | async-start | bytes 2097152 | tf_op jit(solution)/shard_map/all_to_all | solution.py:322
  94.8 0.5 broadcast.46
  95.3 0.8 reduce.5
  96.1 0.1 all_to_all.16
  96.3 16.4 %all-to-all-done.1 = bf16[128,12,256]{2,1,0:T(8,128)(2,1)S(1)} async-done(((bf16[128,12,256]{2,1,0:T(8,128)(2,1)}), bf16[128,12,256]{2,1,0:T(8,128)(2,1)S(1)}, u32[]{:S(2)}, u32[]{:S(2)}) %all-to-all-start.1) | async-done | bytes 786464 | tf_op jit(solution)/shard_map/all_to_all | solution.py:322
  112.7 0.2 reshape.73
  112.8 15.5 %scatter_custom_fusion.2 = f32[16384,256]{1,0:T(8,128)} fusion(s32[1536]{0:T(1024)S(1)} %fusion.6, f32[1536,256]{1,0:T(8,128)S(1)} %reshape.73, f32[]{:T(128)} %constant.6.clone.1), kind=kCustom, calls=%fused_computation.3 | custom fusion | flops 393216 | bytes 16777220 | tf_op jit(solution)/shard_map/scatter-add | solution.py:328
  128.4 0.0 copy-start.1
  128.4 0.0 copy-start
  128.4 9.0 %convert_element_type.28 = bf16[16384,256]{1,0:T(8,128)(2,1)} convert(f32[16384,256]{1,0:T(8,128)} %scatter_custom_fusion.2) | non-fusion elementwise | flops 4194304 | bytes 25165824 | tf_op jit(solution)/shard_map/convert_element_type | solution.py:329
  137.4 0.0 copy-done.1
  137.4 0.7 copy.11
  138.1 0.0 copy-done
  138.1 0.7 copy.12
  (2 shorter events, 0.0 us)
Async XLA Ops:
  5.7 80.7 %all-to-all-start = ((s32[128,12,1]{1,2,0:T(1,128)}), s32[128,12,1]{1,2,0:T(1,128)S(1)}, u32[]{:S(2)}, u32[]{:S(2)}) async-start(s32[128,12,1]{1,2,0:T(1,128)} %bitcast.4), calls=%async_computation | async-start | bytes 131072 | tf_op jit(solution)/shard_map/all_to_all | solution.py:323
  86.5 26.2 %all-to-all-start.1 = ((bf16[128,12,256]{2,1,0:T(8,128)(2,1)}), bf16[128,12,256]{2,1,0:T(8,128)(2,1)S(1)}, u32[]{:S(2)}, u32[]{:S(2)}) async-start(bf16[128,12,256]{2,1,0:T(8,128)(2,1)} %all_to_all.17), calls=%async_computation.1 | async-start | bytes 2097152 | tf_op jit(solution)/shard_map/all_to_all | solution.py:322
  128.4 9.0 %copy-start.1 = (bf16[512,256]{1,0:T(8,128)(2,1)S(1)}, bf16[512,256]{1,0:T(8,128)(2,1)}, u32[]{:S(2)}) copy-start(bf16[512,256]{1,0:T(8,128)(2,1)} %get-tuple-element.10) | copy-start | bytes 786436
  128.4 9.7 %copy-start = (bf16[512,256]{1,0:T(8,128)(2,1)S(1)}, bf16[512,256]{1,0:T(8,128)(2,1)}, u32[]{:S(2)}) copy-start(bf16[512,256]{1,0:T(8,128)(2,1)} %get-tuple-element.11) | copy-start | bytes 786436
